TPU v7x, 128 devices: a whole 4x4x4 slice. The times are simulated.
128 devices in a mesh: row: 8 (over y, x_lo), col: 16 (over z, x_hi, core).
Axes of the slice: x: 4 (x_hi: 2, x_lo: 2; x = x_hi * 2 + x_lo), y: 4, z: 4, core: 2. Of those that a mesh axis runs over, the one named last changes fastest.
Arguments:
- gains: float32 [512, 8, 256], P(('row', 'col')), may hold values from -6 to 6
- coherency: bfloat16 [512, 512, 8, 1, 256], P('row', 'col'), may hold values from -6 to 6
- cotangent: bfloat16 [512, 512, 8, 1, 8], P('row', 'col'), may hold values from -0.099609375 to 0.099609375
- flags: int32 [512, 512, 1], P('row', 'col'), may hold values 0 or 1
- station_slot: int32 [512], replicated, may hold values from 0 to 511, as said below
Outputs:
- gain_grad: float32 [512, 8, 256], P(('row', 'col'))
Inputs may be any that keep to these rules, and one draw needn't show every extreme that they name: `station_slot`: each station appears in exactly one slot; in every aligned block of 4 consecutive slots the stations lie with 4 different holders, station s being held by the device of index s // 4 in the order of row+col.
All inputs are finite; a program needn't handle non-finite values. No bound on the sum of `flags` on one device may be relied on, other than what follows from the above.
Results may differ from a plain program's by a relative error of at most 0.0003.
Values sent between devices are 32-bit elements; how exact they have to be, the bound alone decides.
No kernel may reach another device: no remote copies, remote signals or barrier semaphores. Data moves between devices by JAX's collectives and lax.ppermute only.
A program may use at most 128 MiB of HBM per device.

v0:
```python
import jax
import jax.numpy as jnp
from jax import lax
from jax.sharding import PartitionSpec as P


def laid_out(blocks, dim):
    dims = list(blocks.shape[1:])
    dims[dim] *= blocks.shape[0]
    return jnp.moveaxis(blocks, 0, dim).reshape(dims)


def copy_for_each(x, axis):
    copies = jnp.broadcast_to(x, (lax.axis_size(axis), *x.shape))
    return lax.all_to_all(copies, axis, split_axis=0, concat_axis=0, tiled=True)


def gathered_copies(x, axis, dim):
    return laid_out(copy_for_each(x, axis), dim)


def split_up(x, dim, length):
    before, after = (x.shape[:dim], x.shape[dim + 1 :])
    return jnp.moveaxis(x.reshape(*before, length, -1, *after), dim, 0)


def summed_on_arrival(x, axis, dim):
    blocks = split_up(x, dim, lax.axis_size(axis))
    arrived = lax.all_to_all(blocks, axis, split_axis=0, concat_axis=0, tiled=True)
    return arrived.sum(axis=0)


def side_by_side(arrays, axis, split_dim, concat_dim, along):
    ends, at = ([], 0)
    for a in arrays[:-1]:
        at += a.shape[along]
        ends.append(at)
    both = jnp.concatenate(arrays, axis=along)
    return tuple(
        jnp.split(
            lax.all_to_all(both, axis, split_axis=split_dim, concat_axis=concat_dim, tiled=True),
            ends,
            axis=along,
        )
    )


def complex_product(first, second):
    return (
        first[0] * second[0] - first[1] * second[1],
        first[0] * second[1] + first[1] * second[0],
    )


def complex_sum(first, second):
    return (first[0] + second[0], first[1] + second[1])


def conjugate(element):
    return (element[0], -element[1])


def jones_product(first, second):
    return [
        complex_sum(
            complex_product(first[2 * row_index], second[column]),
            complex_product(first[2 * row_index + 1], second[2 + column]),
        )
        for row_index in (0, 1)
        for column in (0, 1)
    ]


def hermitian(matrix):
    return [conjugate(matrix[0]), conjugate(matrix[2]), conjugate(matrix[1]), conjugate(matrix[3])]


def as_complex(parts):
    return [(parts[0], parts[1]), (parts[2], parts[3]), (parts[4], parts[5]), (parts[6], parts[7])]


def as_parts(matrix):
    return [number for element in matrix for number in element]


def block_gradients(coherency, cotangent, flags, row_gains, col_gains):
    shape = coherency.shape
    directions = shape[4] // 8
    coherence = coherency.reshape(shape[:4] + (8, directions))
    weight = flags.astype(jnp.float32)[:, :, None, :, None]
    residual = as_complex(
        [
            cotangent[..., component].astype(jnp.float32)[..., None] * weight
            for component in range(8)
        ]
    )
    model_parts = as_complex(
        [coherence[..., component, :].astype(jnp.float32) for component in range(8)]
    )
    row_split = row_gains.reshape(row_gains.shape[0], row_gains.shape[1], 8, directions)
    col_split = col_gains.reshape(col_gains.shape[0], col_gains.shape[1], 8, directions)
    row_jones = as_complex([row_split[:, None, :, None, component, :] for component in range(8)])
    col_jones = as_complex([col_split[None, :, :, None, component, :] for component in range(8)])
    outgoing = jones_product(jones_product(residual, col_jones), hermitian(model_parts))
    row_side = jnp.stack([jnp.sum(part, axis=(1, 3)) for part in as_parts(outgoing)], axis=2)
    incoming = jones_product(jones_product(hermitian(residual), row_jones), model_parts)
    col_side = jnp.stack([jnp.sum(part, axis=(0, 3)) for part in as_parts(incoming)], axis=2)
    return (row_side.reshape(row_gains.shape), col_side.reshape(col_gains.shape))


def selector(identifiers, count):
    return (identifiers[:, None] == jnp.arange(count, dtype=jnp.int32)[None, :]).astype(jnp.float32)


def select_rows(table, values):
    return jnp.dot(
        table, values, precision=lax.Precision.HIGHEST, preferred_element_type=jnp.float32
    )


def shards(gains, coherency, cotangent, flags, station_slot):
    stations = station_slot.shape[0]
    share = gains.shape[0]
    flat = gains.shape[1] * gains.shape[2]
    row_total = lax.axis_size("row")
    col_total = lax.axis_size("col")
    groups = row_total * col_total
    row_place = lax.axis_index("row")
    col_place = lax.axis_index("col")
    device_place = row_place * col_total + col_place
    counting = jnp.arange(share, dtype=jnp.int32)
    slot_of = (
        jnp.zeros((stations,), jnp.int32)
        .at[station_slot]
        .set(jnp.arange(stations, dtype=jnp.int32))
    )
    own_blocks = jnp.take(slot_of, device_place * share + counting) // share
    col_target = own_blocks % row_total * col_total + own_blocks // row_total
    col_block = col_place * row_total + row_place
    row_holder = jnp.take(station_slot, device_place * share + counting) // share
    col_holder = jnp.take(station_slot, col_block * share + counting) // share
    row_count = coherency.shape[0]
    col_count = coherency.shape[1]
    row_ids = lax.dynamic_slice_in_dim(station_slot, row_place * row_count, row_count)
    col_ids = lax.dynamic_slice_in_dim(station_slot, col_place * col_count, col_count)
    col_piece = gathered_copies(gains, "col", 0)
    every_gain = lax.all_gather(col_piece, "row", axis=0, tiled=True)
    row_gains = jnp.take(every_gain, row_ids, axis=0)
    col_gains = jnp.take(every_gain, col_ids, axis=0)
    row_side, col_side = block_gradients(coherency, cotangent, flags, row_gains, col_gains)
    row_sum = summed_on_arrival(row_side, "col", 0)
    col_sum = summed_on_arrival(col_side, "row", 0)
    back_row = select_rows(selector(row_holder, groups).T, row_sum.reshape(share, flat))
    back_col = select_rows(selector(col_holder, groups).T, col_sum.reshape(share, flat))
    recv_row, recv_col = side_by_side((back_row, back_col), ("row", "col"), 0, 0, 1)
    result = select_rows(selector(own_blocks, groups), recv_row) + select_rows(
        selector(col_target, groups), recv_col
    )
    return result.reshape(gains.shape)


def solution(mesh):
    placed = (
        P(("row", "col"), None, None),
        P("row", "col", None, None, None),
        P("row", "col", None, None, None),
        P("row", "col", None),
        P(),
    )
    return jax.shard_map(
        shards, mesh=mesh, in_specs=placed, out_specs=P(("row", "col"), None, None), check_vma=False
    )
```

profile of v0, /device:TPU:1, one launch (start us, length us, event | category | flops | bytes accessed | tf_op | source)
XLA Modules:
  0.0 348.7 jit_solution(1977223666826343122)
XLA Ops:
  6.5 0.8 broadcast_in_dim.52
  7.3 20.3 %all_to_all.27 = f32[16,4,8,256]{3,2,1,0:T(8,128)} all-to-all(f32[16,4,8,256]{3,2,1,0:T(8,128)S(1)} %broadcast_in_dim.52), channel_id=1, replica_groups=mesh['row'=8,'col'=16] {'col'}, dimensions={0} | all-to-all | bytes 1048576 | tf_op jit(solution)/shard_map/all_to_all | solution.py:15
  27.7 0.7 convert_element_type.404
  28.5 17.5 %copy.42 = bf16[64,32,8,1,256]{0,4,2,1,3:T(8,128)(2,1)} copy(bf16[64,32,8,1,256]{4,2,3,1,0:T(8,128)(2,1)} %param.8) | data formatting | bytes 16777216 | tf_op args[1]
  46.0 0.6 gather_fusion.4
  46.8 1.4 fusion.93
  48.3 67.3 %all-gather.2.cloned.1.call-done = f32[512,8,256]{2,1,0:T(8,128)} async-done(((f32[64,8,256]{2,1,0:T(8,128)}), f32[512,8,256]{2,1,0:T(8,128)}) %all-gather.2.cloned.1.call-update) | async-done | bytes 4194320 | tf_op jit(solution)/shard_map/all_gather | solution.py:147
  115.5 2.8 gather_fusion.1
  118.3 0.4 copy.51
  118.9 8.5 %fusion.69 = f32[32,8,32]{2,1,0:T(8,128)S(1)} fusion(f32[64,8,32]{0,2,1:T(8,128)S(1)} %get-tuple-element.29, f32[64,8,32]{0,2,1:T(8,128)S(1)} %get-tuple-element.30, f32[64,8,32]{0,2,1:T(8,128)S(1)} %get-tuple-element.31, f32[64,8,32]{0,2,1:T(8,128)S(1)} %get-tuple-element.32, f32[64,8,32]{0,2,1:T(8,128)S(1)} %get-tuple-element.33, ...), kind=kLoop, calls=%fused_computation.127 | loop fusion | flops 20963328 | bytes 5013504 | tf_op jit(solution)/shard_map/reduce_sum | solution.py:107
  127.5 8.5 %fusion.66 = f32[32,8,32]{2,1,0:T(8,128)} fusion(f32[64,8,32]{0,2,1:T(8,128)S(1)} %get-tuple-element.29, f32[64,8,32]{0,2,1:T(8,128)S(1)} %get-tuple-element.30, f32[64,8,32]{0,2,1:T(8,128)S(1)} %get-tuple-element.31, f32[64,8,32]{0,2,1:T(8,128)S(1)} %get-tuple-element.32, f32[64,8,32]{0,2,1:T(8,128)S(1)} %get-tuple-element.33, ...), kind=kLoop, calls=%fused_computation.124 | loop fusion | flops 20963328 | bytes 5013504 | tf_op jit(solution)/shard_map/reduce_sum | solution.py:107
  136.0 6.9 %fusion.53 = f32[32,8,32]{2,1,0:T(8,128)} fusion(f32[64,8,32]{0,2,1:T(8,128)S(1)} %get-tuple-element.29, f32[64,8,32]{0,2,1:T(8,128)S(1)} %get-tuple-element.30, f32[64,8,32]{0,2,1:T(8,128)S(1)} %get-tuple-element.31, f32[64,8,32]{0,2,1:T(8,128)S(1)} %get-tuple-element.32, f32[64,8,32]{0,2,1:T(8,128)S(1)} %get-tuple-element.33, ...), kind=kLoop, calls=%fused_computation.111 | loop fusion | flops 20963328 | bytes 5013504 | tf_op jit(solution)/shard_map/reduce_sum | solution.py:107
  142.9 6.9 %fusion.50 = f32[32,8,32]{2,1,0:T(8,128)} fusion(f32[64,8,32]{0,2,1:T(8,128)S(1)} %get-tuple-element.29, f32[64,8,32]{0,2,1:T(8,128)S(1)} %get-tuple-element.30, f32[64,8,32]{0,2,1:T(8,128)S(1)} %get-tuple-element.31, f32[64,8,32]{0,2,1:T(8,128)S(1)} %get-tuple-element.32, f32[64,8,32]{0,2,1:T(8,128)S(1)} %get-tuple-element.33, ...), kind=kLoop, calls=%fused_computation.108 | loop fusion | flops 20963328 | bytes 5013504 | tf_op jit(solution)/shard_map/reduce_sum | solution.py:107
  149.8 3.4 gather_fusion
  153.2 1.2 gather.16
  154.6 0.7 fusion.97
  155.3 11.8 %fusion.39 = f32[64,8,32]{0,2,1:T(8,128)S(1)} fusion(f32[64,32,8]{0,2,1:T(8,128)S(1)} %bitcast.387, f32[64,32,8]{0,2,1:T(8,128)S(1)} %bitcast.284, f32[64,32,8]{0,2,1:T(8,128)S(1)} %bitcast.383, f32[64,32,8]{0,2,1:T(8,128)S(1)} %bitcast.296, f32[32,8,32]{2,1,0:T(8,128)S(1)} %bitcast.308, f32[32,8,32]{2,1,0:T(8,128)S(1)} %bitcast.316, ...), kind=kLoop, calls=%fused_computation.97 | loop fusion | flops 22003712 | bytes 4784128 | tf_op jit(solution)/shard_map/reduce_sum | solution.py:105
  167.2 11.8 %fusion.36 = f32[64,8,32]{0,2,1:T(8,128)S(1)} fusion(f32[64,32,8]{0,2,1:T(8,128)S(1)} %bitcast.388, f32[64,32,8]{0,2,1:T(8,128)S(1)} %bitcast.285, f32[64,32,8]{0,2,1:T(8,128)S(1)} %bitcast.384, f32[64,32,8]{0,2,1:T(8,128)S(1)} %bitcast.297, f32[32,8,32]{2,1,0:T(8,128)S(1)} %bitcast.309, f32[32,8,32]{2,1,0:T(8,128)S(1)} %bitcast.317, ...), kind=kLoop, calls=%fused_computation.94 | loop fusion | flops 22003712 | bytes 4784128 | tf_op jit(solution)/shard_map/reduce_sum | solution.py:105
  179.0 11.8 %fusion.27 = f32[64,8,32]{0,2,1:T(8,128)S(1)} fusion(f32[64,32,8]{0,2,1:T(8,128)S(1)} %bitcast.389, f32[64,32,8]{0,2,1:T(8,128)S(1)} %bitcast.286, f32[64,32,8]{0,2,1:T(8,128)S(1)} %bitcast.385, f32[64,32,8]{0,2,1:T(8,128)S(1)} %bitcast.298, f32[32,8,32]{2,1,0:T(8,128)S(1)} %bitcast.310, f32[32,8,32]{2,1,0:T(8,128)S(1)} %bitcast.318, ...), kind=kLoop, calls=%fused_computation.85 | loop fusion | flops 22003712 | bytes 4784128 | tf_op jit(solution)/shard_map/reduce_sum | solution.py:105
  190.9 10.1 %fusion.24 = f32[64,8,32]{0,2,1:T(8,128)S(1)} fusion(f32[64,32,8]{0,2,1:T(8,128)S(1)} %bitcast.390, f32[64,32,8]{0,2,1:T(8,128)S(1)} %bitcast.287, f32[64,32,8]{0,2,1:T(8,128)S(1)} %bitcast.386, f32[64,32,8]{0,2,1:T(8,128)S(1)} %bitcast.299, f32[32,8,32]{2,1,0:T(8,128)S(1)} %bitcast.311, f32[32,8,32]{2,1,0:T(8,128)S(1)} %bitcast.319, ...), kind=kLoop, calls=%fused_computation.82 | loop fusion | flops 22003712 | bytes 4784128 | tf_op jit(solution)/shard_map/reduce_sum | solution.py:105
  201.0 10.7 %fusion.33 = f32[64,8,32]{0,2,1:T(8,128)} fusion(f32[32,8,32]{2,1,0:T(8,128)S(1)} %bitcast.312, f32[32,8,32]{2,1,0:T(8,128)S(1)} %bitcast.320, f32[32,8,32]{2,1,0:T(8,128)S(1)} %bitcast.328, f32[32,8,32]{2,1,0:T(8,128)S(1)} %bitcast.336, f32[32,8,32]{2,1,0:T(8,128)S(1)} %bitcast.344, f32[64,32,8]{0,2,1:T(8,128)S(1)} %bitcast.367, ...), kind=kLoop, calls=%fused_computation.91 | loop fusion | flops 22003712 | bytes 4784128 | tf_op jit(solution)/shard_map/reduce_sum | solution.py:105
  211.7 9.9 %fusion.18 = f32[64,8,32]{0,2,1:T(8,128)S(1)} fusion(f32[32,8,32]{2,1,0:T(8,128)S(1)} %bitcast.313, f32[32,8,32]{2,1,0:T(8,128)S(1)} %bitcast.321, f32[32,8,32]{2,1,0:T(8,128)S(1)} %bitcast.329, f32[32,8,32]{2,1,0:T(8,128)S(1)} %bitcast.337, f32[32,8,32]{2,1,0:T(8,128)S(1)} %bitcast.345, f32[64,32,8]{0,2,1:T(8,128)S(1)} %bitcast.368, ...), kind=kLoop, calls=%fused_computation.76 | loop fusion | flops 22003712 | bytes 4784128 | tf_op jit(solution)/shard_map/reduce_sum | solution.py:105
  221.6 6.2 %fusion.56 = f32[32,8,32]{2,1,0:T(8,128)S(1)} fusion(f32[64,32,8]{0,2,1:T(8,128)S(1)} %bitcast.379, f32[64,32,8]{0,2,1:T(8,128)S(1)} %bitcast.375, f32[64,8,32]{0,2,1:T(8,128)S(1)} %get-tuple-element.29, f32[64,8,32]{0,2,1:T(8,128)S(1)} %get-tuple-element.30, f32[64,8,32]{0,2,1:T(8,128)S(1)} %get-tuple-element.31, f32[64,8,32]{0,2,1:T(8,128)S(1)} %get-tuple-element.32, ...), kind=kLoop, calls=%fused_computation.114 | loop fusion | flops 20963328 | bytes 5013504 | tf_op jit(solution)/shard_map/reduce_sum | solution.py:107
  227.8 6.2 %fusion.72 = f32[32,8,32]{2,1,0:T(8,128)S(1)} fusion(f32[64,32,8]{0,2,1:T(8,128)S(1)} %bitcast.380, f32[64,32,8]{0,2,1:T(8,128)S(1)} %bitcast.376, f32[64,8,32]{0,2,1:T(8,128)S(1)} %get-tuple-element.29, f32[64,8,32]{0,2,1:T(8,128)S(1)} %get-tuple-element.30, f32[64,8,32]{0,2,1:T(8,128)S(1)} %get-tuple-element.31, f32[64,8,32]{0,2,1:T(8,128)S(1)} %get-tuple-element.32, ...), kind=kLoop, calls=%fused_computation.130 | loop fusion | flops 20963328 | bytes 5013504 | tf_op jit(solution)/shard_map/reduce_sum | solution.py:107
  234.0 6.2 %fusion.75 = f32[32,8,32]{2,1,0:T(8,128)S(1)} fusion(f32[64,32,8]{0,2,1:T(8,128)S(1)} %bitcast.381, f32[64,32,8]{0,2,1:T(8,128)S(1)} %bitcast.377, f32[64,8,32]{0,2,1:T(8,128)S(1)} %get-tuple-element.29, f32[64,8,32]{0,2,1:T(8,128)S(1)} %get-tuple-element.30, f32[64,8,32]{0,2,1:T(8,128)S(1)} %get-tuple-element.31, f32[64,8,32]{0,2,1:T(8,128)S(1)} %get-tuple-element.32, ...), kind=kLoop, calls=%fused_computation.133 | loop fusion | flops 20963328 | bytes 5013504 | tf_op jit(solution)/shard_map/reduce_sum | solution.py:107
  240.2 6.2 %fusion.59 = f32[32,8,32]{2,1,0:T(8,128)S(1)} fusion(f32[64,32,8]{0,2,1:T(8,128)S(1)} %bitcast.382, f32[64,32,8]{0,2,1:T(8,128)S(1)} %bitcast.378, f32[64,8,32]{0,2,1:T(8,128)S(1)} %get-tuple-element.29, f32[64,8,32]{0,2,1:T(8,128)S(1)} %get-tuple-element.30, f32[64,8,32]{0,2,1:T(8,128)S(1)} %get-tuple-element.31, f32[64,8,32]{0,2,1:T(8,128)S(1)} %get-tuple-element.32, ...), kind=kLoop, calls=%fused_computation.117 | loop fusion | flops 20963328 | bytes 5013504 | tf_op jit(solution)/shard_map/reduce_sum | solution.py:107
  246.5 9.9 %fusion.30 = f32[64,8,32]{0,2,1:T(8,128)S(1)} fusion(f32[32,8,32]{2,1,0:T(8,128)S(1)} %bitcast.314, f32[32,8,32]{2,1,0:T(8,128)S(1)} %bitcast.322, f32[32,8,32]{2,1,0:T(8,128)S(1)} %bitcast.330, f32[32,8,32]{2,1,0:T(8,128)S(1)} %bitcast.338, f32[32,8,32]{2,1,0:T(8,128)S(1)} %bitcast.346, f32[64,32,8]{0,2,1:T(8,128)S(1)} %bitcast.369, ...), kind=kLoop, calls=%fused_computation.88 | loop fusion | flops 22003712 | bytes 4784128 | tf_op jit(solution)/shard_map/reduce_sum | solution.py:105
  256.4 9.9 %fusion.21 = f32[64,8,32]{0,2,1:T(8,128)S(1)} fusion(f32[32,8,32]{2,1,0:T(8,128)S(1)} %bitcast.315, f32[32,8,32]{2,1,0:T(8,128)S(1)} %bitcast.323, f32[32,8,32]{2,1,0:T(8,128)S(1)} %bitcast.331, f32[32,8,32]{2,1,0:T(8,128)S(1)} %bitcast.339, f32[32,8,32]{2,1,0:T(8,128)S(1)} %bitcast.347, f32[64,32,8]{0,2,1:T(8,128)S(1)} %bitcast.370, ...), kind=kLoop, calls=%fused_computation.79 | loop fusion | flops 22003712 | bytes 4784128 | tf_op jit(solution)/shard_map/reduce_sum | solution.py:105
  266.4 1.6 stack.71
  268.0 1.0 reshape_reshape.7
  269.0 3.8 %all-to-all-start.2 = ((f32[8,4,8,256]{3,2,1,0:T(8,128)}), f32[8,4,8,256]{3,2,1,0:T(8,128)S(1)}, u32[]{:S(2)}, u32[]{:S(2)}) async-start(f32[8,4,8,256]{3,2,1,0:T(8,128)} %reshape_reshape.7), calls=%async_computation.2 | async-start | bytes 524288 | tf_op jit(solution)/shard_map/all_to_all | solution.py:29
  273.0 1.8 copy.50
  274.9 1.4 reshape_reshape.6
  276.2 2.8 all-to-all-done.2
  279.0 9.1 %all-to-all-start.1 = ((f32[16,4,8,256]{3,2,1,0:T(8,128)}), f32[16,4,8,256]{3,2,1,0:T(8,128)S(1)}, u32[]{:S(2)}, u32[]{:S(2)}) async-start(f32[16,4,8,256]{3,2,1,0:T(8,128)} %reshape_reshape.6), calls=%async_computation.1 | async-start | bytes 1048576 | tf_op jit(solution)/shard_map/all_to_all | solution.py:29
  288.1 0.6 gather_fusion.3
  288.8 0.7 fusion.84
  289.5 9.7 %all-to-all-done.1 = f32[16,4,8,256]{3,2,1,0:T(8,128)S(1)} async-done(((f32[16,4,8,256]{3,2,1,0:T(8,128)}), f32[16,4,8,256]{3,2,1,0:T(8,128)S(1)}, u32[]{:S(2)}, u32[]{:S(2)}) %all-to-all-start.1) | async-done | bytes 524320 | tf_op jit(solution)/shard_map/all_to_all | solution.py:29
  299.3 0.7 fusion.83
  300.2 3.5 %copy.52 = f32[128,1,4096]{2,1,0:T(1,128)} copy(f32[128,1,4096]{2,0,1:T(8,128)S(1)} %maximum_bitcast_fusion) | data formatting | bytes 4194304 | tf_op jit(solution)/shard_map/all_to_all | solution.py:41
  303.7 4.7 %all-to-all-start.3 = ((f32[128,1,4096]{2,1,0:T(1,128)}), f32[128,1,4096]{2,1,0:T(1,128)S(1)}, u32[]{:S(2)}, u32[]{:S(2)}) async-start(f32[128,1,4096]{2,1,0:T(1,128)} %copy.52), calls=%async_computation.3 | async-start | bytes 4194304 | tf_op jit(solution)/shard_map/all_to_all | solution.py:41
  308.5 2.4 scatter_custom_fusion
  310.9 0.6 gather_fusion.2
  311.6 27.1 %all-to-all-done.3 = f32[128,1,4096]{2,1,0:T(1,128)S(1)} async-done(((f32[128,1,4096]{2,1,0:T(1,128)}), f32[128,1,4096]{2,1,0:T(1,128)S(1)}, u32[]{:S(2)}, u32[]{:S(2)}) %all-to-all-start.3) | async-done | bytes 2097184 | tf_op jit(solution)/shard_map/all_to_all | solution.py:41
  338.7 1.6 copy.66
  340.3 0.5 fusion.81
  340.8 0.5 convolution_add_fusion
  341.2 0.6 copy.67
  (52 shorter events, 1.0 us)
Async XLA Ops:
  6.5 109.0 %all-gather.2.cloned.1.call-start = ((), (), s32[]{:S(2)}) async-start(), calls=%async_computation.4 | async-start | bytes 4718592 | tf_op jit(solution)/shard_map/all_gather | solution.py:147
  28.5 17.6 %copy-start.1 = (s32[512]{0:T(512)S(1)}, s32[512]{0:T(512)}, u32[]{:S(2)}) copy-start(s32[512]{0:T(512)} %param.11) | copy-start | bytes 6148
  28.5 18.4 %copy-start.2 = (bf16[64,32,8,1,8]{0,4,3,2,1:T(8,128)(2,1)S(1)}, bf16[64,32,8,1,8]{0,4,3,2,1:T(8,128)(2,1)}, u32[]{:S(2)}) copy-start(bf16[64,32,8,1,8]{0,4,3,2,1:T(8,128)(2,1)} %param.9) | copy-start | bytes 786436
  118.9 17.0 %copy-start = (bf16[64,32,8,1,256]{0,4,2,1,3:T(8,128)(2,1)S(1)}, bf16[64,32,8,1,256]{0,4,2,1,3:T(8,128)(2,1)}, u32[]{:S(2)}) copy-start(bf16[64,32,8,1,256]{0,4,2,1,3:T(8,128)(2,1)} %copy.42) | copy-start | bytes 25165828
  155.3 35.6 %slice-start = ((s8[16777216]{0:T(1024)(128)(4,1)}), s8[4194304]{0:T(1024)(128)(4,1)S(1)}, s32[]{:S(2)}) async-start(s8[16777216]{0:T(1024)(128)(4,1)} %bitcast.257), calls=%async_computation.5 | async-start | bytes 8388608
  155.3 35.6 %slice-start.1 = ((s8[16777216]{0:T(1024)(128)(4,1)}), s8[4194304]{0:T(1024)(128)(4,1)S(1)}, s32[]{:S(2)}) async-start(s8[16777216]{0:T(1024)(128)(4,1)} %bitcast.257), calls=%async_computation.6 | async-start | bytes 8388608
  167.2 23.7 %slice-start.2 = ((s8[16777216]{0:T(1024)(128)(4,1)}), s8[4194304]{0:T(1024)(128)(4,1)S(1)}, s32[]{:S(2)}) async-start(s8[16777216]{0:T(1024)(128)(4,1)} %bitcast.257), calls=%async_computation.7 | async-start | bytes 8388608
  179.0 11.9 %slice-start.3 = ((s8[16777216]{0:T(1024)(128)(4,1)}), s8[4194304]{0:T(1024)(128)(4,1)S(1)}, s32[]{:S(2)}) async-start(s8[16777216]{0:T(1024)(128)(4,1)} %bitcast.257), calls=%async_computation.8 | async-start | bytes 8388608
  256.4 10.0 %copy-start.3 = (f32[32,8,32]{2,1,0:T(8,128)S(1)}, f32[32,8,32]{2,1,0:T(8,128)}, u32[]{:S(2)}) copy-start(f32[32,8,32]{2,1,0:T(8,128)} %fusion.66) | copy-start | bytes 98308
  256.4 10.0 %copy-start.4 = (f32[32,8,32]{2,1,0:T(8,128)S(1)}, f32[32,8,32]{2,1,0:T(8,128)}, u32[]{:S(2)}) copy-start(f32[32,8,32]{2,1,0:T(8,128)} %fusion.53) | copy-start | bytes 98308
  256.4 10.0 %copy-start.5 = (f32[32,8,32]{2,1,0:T(8,128)S(1)}, f32[32,8,32]{2,1,0:T(8,128)}, u32[]{:S(2)}) copy-start(f32[32,8,32]{2,1,0:T(8,128)} %fusion.50) | copy-start | bytes 98308
  266.4 6.5 %copy-start.6 = (f32[64,8,32]{0,2,1:T(8,128)S(1)}, f32[64,8,32]{0,2,1:T(8,128)}, u32[]{:S(2)}) copy-start(f32[64,8,32]{0,2,1:T(8,128)} %fusion.33) | copy-start | bytes 196612
  269.0 10.0 %all-to-all-start.2 = ((f32[8,4,8,256]{3,2,1,0:T(8,128)}), f32[8,4,8,256]{3,2,1,0:T(8,128)S(1)}, u32[]{:S(2)}, u32[]{:S(2)}) async-start(f32[8,4,8,256]{3,2,1,0:T(8,128)} %reshape_reshape.7), calls=%async_computation.2 | async-start | bytes 524288 | tf_op jit(solution)/shard_map/all_to_all | solution.py:29
  279.0 20.2 %all-to-all-start.1 = ((f32[16,4,8,256]{3,2,1,0:T(8,128)}), f32[16,4,8,256]{3,2,1,0:T(8,128)S(1)}, u32[]{:S(2)}, u32[]{:S(2)}) async-start(f32[16,4,8,256]{3,2,1,0:T(8,128)} %reshape_reshape.6), calls=%async_computation.1 | async-start | bytes 1048576 | tf_op jit(solution)/shard_map/all_to_all | solution.py:29
  303.7 34.9 %all-to-all-start.3 = ((f32[128,1,4096]{2,1,0:T(1,128)}), f32[128,1,4096]{2,1,0:T(1,128)S(1)}, u32[]{:S(2)}, u32[]{:S(2)}) async-start(f32[128,1,4096]{2,1,0:T(1,128)} %copy.52), calls=%async_computation.3 | async-start | bytes 4194304 | tf_op jit(solution)/shard_map/all_to_all | solution.py:41
Sparse Core Ops, SparseCore 0:
  27.8 87.6 all-gather.1
where the time goes:
time: 350 us; the launch traced here: 349 us
  other arithmetic  145 us (41%)
  waiting for transfers between devices  107 us (31%)
  local copies, waits for them, and re-layouts  43.1 us (12%)
  blocking collectives  20.3 us (6%)
  starting transfers between devices  17.6 us (5%)
  between operations  13.9 us (4%)
    reduce_sum x8, other arithmetic, block_gradients(): jnp.sum(part, axis=(1, 3))  86.1 us
    all_gather x1, waiting for transfers between devices, shards(): every_gain = lax.all_gather(col_piece, 'row', axis=0, tiled=True)  67.3 us
    reduce_sum x8, other arithmetic, block_gradients(): jnp.sum(part, axis=(0, 3))  55.6 us
    all_to_all x1, waiting for transfers between devices, side_by_side(): lax.all_to_all(both, axis, split_axis=split_dim, concat_axis=concat_dim,...  27.1 us
    all_to_all x1, blocking collectives, copy_for_each(): return lax.all_to_all(copies, axis, split_axis=0, concat_axis=0, tiled=True)  20.3 us
    unnamed x34, local copies, waits for them, and re-layouts  19.9 us
    all_to_all x2, starting transfers between devices, summed_on_arrival(): lax.all_to_all(blocks, axis, split_axis=0, concat_axis=0, tiled=True)  12.9 us
    all_to_all x2, waiting for transfers between devices, summed_on_arrival(): lax.all_to_all(blocks, axis, split_axis=0, concat_axis=0, tiled=True)  12.5 us
  transfers between devices with their start and end apart: 4, of which 4 were waited for; matrix products, arithmetic and copies ran while one was open for 8% of the time, Pallas kernels for 0%

commit v1 on v0

--- a/solution.py
+++ b/solution.py
@@ -144,7 +144,9 @@
     row_ids = lax.dynamic_slice_in_dim(station_slot, row_place * row_count, row_count)
     col_ids = lax.dynamic_slice_in_dim(station_slot, col_place * col_count, col_count)
     col_piece = gathered_copies(gains, "col", 0)
-    every_gain = lax.all_gather(col_piece, "row", axis=0, tiled=True)
+    every_gain = jnp.concatenate(
+        lax.all_to_all(jnp.stack([col_piece] * lax.axis_size("row")), "row", 0, 0), axis=0
+    )
     row_gains = jnp.take(every_gain, row_ids, axis=0)
     col_gains = jnp.take(every_gain, col_ids, axis=0)
     row_side, col_side = block_gradients(coherency, cotangent, flags, row_gains, col_gains)

time: 350 us -> 305 us (0.87)
  waiting for transfers between devices: 107 us -> 65.2 us
  between operations: 13.9 us -> 0.46 us
  local copies, waits for them, and re-layouts: 43.1 us -> 48.1 us
    all_gather x1 -> x0, waiting for transfers between devices: 67.3 us -> none  [shards(): every_gain = lax.all_gather(col_piece, 'row', axis=0, tiled=True)]
    all_to_all x0 -> x1, waiting for transfers between devices: none -> 28.4 us  [shards(): lax.all_to_all(jnp.stack([col_piece] * lax.axis_size('row')), 'row', 0, 0)]
    all_to_all x0 -> x1, starting transfers between devices: none -> 4.68 us  [shards(): lax.all_to_all(jnp.stack([col_piece] * lax.axis_size('row')), 'row', 0, 0)]
    reduce_sum x8, other arithmetic: 86.1 us -> 89.8 us  [block_gradients(): jnp.sum(part, axis=(1, 3))]
    unnamed x34 -> x40, local copies, waits for them, and re-layouts: 19.9 us -> 22.6 us
  transfers between devices with their start and end apart: 4 -> 4, of which waited for: 4 -> 4; matrix products, arithmetic and copies ran while one was open for 8% -> 10% of each run, Pallas kernels for 0% -> 0%
where the time goes in v1:
time: 305 us; the launch traced here: 304 us
  other arithmetic  148 us (49%)
  waiting for transfers between devices  65.2 us (21%)
  local copies, waits for them, and re-layouts  48.1 us (16%)
  starting transfers between devices  20.3 us (7%)
  blocking collectives  20.2 us (7%)
    reduce_sum x8, other arithmetic, block_gradients(): jnp.sum(part, axis=(1, 3))  89.8 us
    reduce_sum x8, other arithmetic, block_gradients(): jnp.sum(part, axis=(0, 3))  55.6 us
    all_to_all x1, waiting for transfers between devices, shards(): lax.all_to_all(jnp.stack([col_piece] * lax.axis_size('row')), 'row', 0, 0)  28.4 us
    all_to_all x1, waiting for transfers between devices, side_by_side(): lax.all_to_all(both, axis, split_axis=split_dim, concat_axis=concat_dim,...  27 us
    unnamed x40, local copies, waits for them, and re-layouts  22.6 us
    all_to_all x1, blocking collectives, copy_for_each(): return lax.all_to_all(copies, axis, split_axis=0, concat_axis=0, tiled=True)  20.2 us
    all_to_all x2, starting transfers between devices, summed_on_arrival(): lax.all_to_all(blocks, axis, split_axis=0, concat_axis=0, tiled=True)  10.2 us
    all_to_all x2, waiting for transfers between devices, summed_on_arrival(): lax.all_to_all(blocks, axis, split_axis=0, concat_axis=0, tiled=True)  9.88 us
  transfers between devices with their start and end apart: 4, of which 4 were waited for; matrix products, arithmetic and copies ran while one was open for 10% of the time, Pallas kernels for 0%

profile of v1, /device:TPU:1, one launch (start us, length us, event | category | flops | bytes accessed | tf_op | source)
XLA Modules:
  0.0 304.2 jit_solution(10075224547568082969)
XLA Ops:
  0.0 0.8 broadcast_in_dim.52
  0.8 20.2 %all_to_all.32 = f32[16,4,8,256]{3,2,1,0:T(8,128)S(1)} all-to-all(f32[16,4,8,256]{3,2,1,0:T(8,128)S(1)} %broadcast_in_dim.52), channel_id=1, replica_groups=mesh['row'=8,'col'=16] {'col'}, dimensions={0} | all-to-all | bytes 1048576 | tf_op jit(solution)/shard_map/all_to_all | solution.py:15
  21.0 2.3 stack.57
  23.4 4.7 %all-to-all-start.1 = ((f32[8,64,8,256]{3,2,1,0:T(8,128)}), f32[8,64,8,256]{3,2,1,0:T(8,128)}, u32[]{:S(2)}, u32[]{:S(2)}) async-start(f32[8,64,8,256]{3,2,1,0:T(8,128)} %stack.57), calls=%async_computation.1 | async-start | bytes 8388608 | tf_op jit(solution)/shard_map/all_to_all | solution.py:148
  28.1 17.5 %copy.42 = bf16[64,32,8,1,256]{0,4,2,1,3:T(8,128)(2,1)} copy(bf16[64,32,8,1,256]{4,2,3,1,0:T(8,128)(2,1)} %param.8) | data formatting | bytes 16777216 | tf_op args[1]
  45.7 0.6 gather_fusion.4
  46.5 1.4 fusion.93
  47.9 28.4 %all-to-all-done.1 = f32[8,64,8,256]{3,2,1,0:T(8,128)} async-done(((f32[8,64,8,256]{3,2,1,0:T(8,128)}), f32[8,64,8,256]{3,2,1,0:T(8,128)}, u32[]{:S(2)}, u32[]{:S(2)}) %all-to-all-start.1) | async-done | bytes 4194336 | tf_op jit(solution)/shard_map/all_to_all | solution.py:148
  76.3 2.8 gather_fusion.1
  79.7 8.5 %fusion.69 = f32[32,8,32]{2,1,0:T(8,128)S(1)} fusion(f32[64,8,32]{0,2,1:T(8,128)S(1)} %get-tuple-element.29, f32[64,8,32]{0,2,1:T(8,128)S(1)} %get-tuple-element.30, f32[64,8,32]{0,2,1:T(8,128)S(1)} %get-tuple-element.31, f32[64,8,32]{0,2,1:T(8,128)S(1)} %get-tuple-element.32, f32[64,8,32]{0,2,1:T(8,128)S(1)} %get-tuple-element.33, ...), kind=kLoop, calls=%fused_computation.127 | loop fusion | flops 20963328 | bytes 5013504 | tf_op jit(solution)/shard_map/reduce_sum | solution.py:107
  88.2 8.5 %fusion.66 = f32[32,8,32]{2,1,0:T(8,128)} fusion(f32[64,8,32]{0,2,1:T(8,128)S(1)} %get-tuple-element.29, f32[64,8,32]{0,2,1:T(8,128)S(1)} %get-tuple-element.30, f32[64,8,32]{0,2,1:T(8,128)S(1)} %get-tuple-element.31, f32[64,8,32]{0,2,1:T(8,128)S(1)} %get-tuple-element.32, f32[64,8,32]{0,2,1:T(8,128)S(1)} %get-tuple-element.33, ...), kind=kLoop, calls=%fused_computation.124 | loop fusion | flops 20963328 | bytes 5013504 | tf_op jit(solution)/shard_map/reduce_sum | solution.py:107
  96.7 6.9 %fusion.53 = f32[32,8,32]{2,1,0:T(8,128)} fusion(f32[64,8,32]{0,2,1:T(8,128)S(1)} %get-tuple-element.29, f32[64,8,32]{0,2,1:T(8,128)S(1)} %get-tuple-element.30, f32[64,8,32]{0,2,1:T(8,128)S(1)} %get-tuple-element.31, f32[64,8,32]{0,2,1:T(8,128)S(1)} %get-tuple-element.32, f32[64,8,32]{0,2,1:T(8,128)S(1)} %get-tuple-element.33, ...), kind=kLoop, calls=%fused_computation.111 | loop fusion | flops 20963328 | bytes 5013504 | tf_op jit(solution)/shard_map/reduce_sum | solution.py:107
  103.7 6.9 %fusion.50 = f32[32,8,32]{2,1,0:T(8,128)} fusion(f32[64,8,32]{0,2,1:T(8,128)S(1)} %get-tuple-element.29, f32[64,8,32]{0,2,1:T(8,128)S(1)} %get-tuple-element.30, f32[64,8,32]{0,2,1:T(8,128)S(1)} %get-tuple-element.31, f32[64,8,32]{0,2,1:T(8,128)S(1)} %get-tuple-element.32, f32[64,8,32]{0,2,1:T(8,128)S(1)} %get-tuple-element.33, ...), kind=kLoop, calls=%fused_computation.108 | loop fusion | flops 20963328 | bytes 5013504 | tf_op jit(solution)/shard_map/reduce_sum | solution.py:107
  110.6 3.4 %gather_fusion = f32[32,8,256]{2,1,0:T(8,128)} fusion(f32[512,8,256]{2,1,0:T(8,128)} %bitcast.3, s32[1024]{0:T(1024)S(1)} %get-tuple-element.49), kind=kCustom, calls=%fused_computation.3 | custom fusion | bytes 524416 | tf_op jit(solution)/shard_map/jit(_take)/gather | solution.py:151
  114.0 1.2 gather.16
  115.4 0.7 fusion.97
  116.1 11.8 %fusion.39 = f32[64,8,32]{0,2,1:T(8,128)S(1)} fusion(f32[64,32,8]{0,2,1:T(8,128)S(1)} %bitcast.388, f32[64,32,8]{0,2,1:T(8,128)S(1)} %bitcast.285, f32[64,32,8]{0,2,1:T(8,128)S(1)} %bitcast.384, f32[64,32,8]{0,2,1:T(8,128)S(1)} %bitcast.297, f32[32,8,32]{2,1,0:T(8,128)S(1)} %bitcast.309, f32[32,8,32]{2,1,0:T(8,128)S(1)} %bitcast.317, ...), kind=kLoop, calls=%fused_computation.97 | loop fusion | flops 22003712 | bytes 4784128 | tf_op jit(solution)/shard_map/reduce_sum | solution.py:105
  128.0 12.4 %fusion.36 = f32[64,8,32]{0,2,1:T(8,128)} fusion(f32[64,32,8]{0,2,1:T(8,128)S(1)} %bitcast.389, f32[64,32,8]{0,2,1:T(8,128)S(1)} %bitcast.286, f32[64,32,8]{0,2,1:T(8,128)S(1)} %bitcast.385, f32[64,32,8]{0,2,1:T(8,128)S(1)} %bitcast.298, f32[32,8,32]{2,1,0:T(8,128)S(1)} %bitcast.310, f32[32,8,32]{2,1,0:T(8,128)S(1)} %bitcast.318, ...), kind=kLoop, calls=%fused_computation.94 | loop fusion | flops 22003712 | bytes 4784128 | tf_op jit(solution)/shard_map/reduce_sum | solution.py:105
  140.4 11.8 %fusion.27 = f32[64,8,32]{0,2,1:T(8,128)S(1)} fusion(f32[64,32,8]{0,2,1:T(8,128)S(1)} %bitcast.390, f32[64,32,8]{0,2,1:T(8,128)S(1)} %bitcast.287, f32[64,32,8]{0,2,1:T(8,128)S(1)} %bitcast.386, f32[64,32,8]{0,2,1:T(8,128)S(1)} %bitcast.299, f32[32,8,32]{2,1,0:T(8,128)S(1)} %bitcast.311, f32[32,8,32]{2,1,0:T(8,128)S(1)} %bitcast.319, ...), kind=kLoop, calls=%fused_computation.85 | loop fusion | flops 22003712 | bytes 4784128 | tf_op jit(solution)/shard_map/reduce_sum | solution.py:105
  152.3 10.9 %fusion.24 = f32[64,8,32]{0,2,1:T(8,128)} fusion(f32[64,32,8]{0,2,1:T(8,128)S(1)} %bitcast.391, f32[64,32,8]{0,2,1:T(8,128)S(1)} %bitcast.288, f32[64,32,8]{0,2,1:T(8,128)S(1)} %bitcast.387, f32[64,32,8]{0,2,1:T(8,128)S(1)} %bitcast.300, f32[32,8,32]{2,1,0:T(8,128)S(1)} %bitcast.312, f32[32,8,32]{2,1,0:T(8,128)S(1)} %bitcast.320, ...), kind=kLoop, calls=%fused_computation.82 | loop fusion | flops 22003712 | bytes 4784128 | tf_op jit(solution)/shard_map/reduce_sum | solution.py:105
  163.1 10.7 %fusion.33 = f32[64,8,32]{0,2,1:T(8,128)} fusion(f32[32,8,32]{2,1,0:T(8,128)S(1)} %bitcast.313, f32[32,8,32]{2,1,0:T(8,128)S(1)} %bitcast.321, f32[32,8,32]{2,1,0:T(8,128)S(1)} %bitcast.329, f32[32,8,32]{2,1,0:T(8,128)S(1)} %bitcast.337, f32[32,8,32]{2,1,0:T(8,128)S(1)} %bitcast.345, f32[64,32,8]{0,2,1:T(8,128)S(1)} %bitcast.368, ...), kind=kLoop, calls=%fused_computation.91 | loop fusion | flops 22003712 | bytes 4784128 | tf_op jit(solution)/shard_map/reduce_sum | solution.py:105
  173.8 10.7 %fusion.18 = f32[64,8,32]{0,2,1:T(8,128)} fusion(f32[32,8,32]{2,1,0:T(8,128)S(1)} %bitcast.314, f32[32,8,32]{2,1,0:T(8,128)S(1)} %bitcast.322, f32[32,8,32]{2,1,0:T(8,128)S(1)} %bitcast.330, f32[32,8,32]{2,1,0:T(8,128)S(1)} %bitcast.338, f32[32,8,32]{2,1,0:T(8,128)S(1)} %bitcast.346, f32[64,32,8]{0,2,1:T(8,128)S(1)} %bitcast.369, ...), kind=kLoop, calls=%fused_computation.76 | loop fusion | flops 22003712 | bytes 4784128 | tf_op jit(solution)/shard_map/reduce_sum | solution.py:105
  184.5 6.2 %fusion.56 = f32[32,8,32]{2,1,0:T(8,128)S(1)} fusion(f32[64,32,8]{0,2,1:T(8,128)S(1)} %bitcast.380, f32[64,32,8]{0,2,1:T(8,128)S(1)} %bitcast.376, f32[64,8,32]{0,2,1:T(8,128)S(1)} %get-tuple-element.29, f32[64,8,32]{0,2,1:T(8,128)S(1)} %get-tuple-element.30, f32[64,8,32]{0,2,1:T(8,128)S(1)} %get-tuple-element.31, f32[64,8,32]{0,2,1:T(8,128)S(1)} %get-tuple-element.32, ...), kind=kLoop, calls=%fused_computation.114 | loop fusion | flops 20963328 | bytes 5013504 | tf_op jit(solution)/shard_map/reduce_sum | solution.py:107
  190.7 6.2 %fusion.72 = f32[32,8,32]{2,1,0:T(8,128)S(1)} fusion(f32[64,32,8]{0,2,1:T(8,128)S(1)} %bitcast.381, f32[64,32,8]{0,2,1:T(8,128)S(1)} %bitcast.377, f32[64,8,32]{0,2,1:T(8,128)S(1)} %get-tuple-element.29, f32[64,8,32]{0,2,1:T(8,128)S(1)} %get-tuple-element.30, f32[64,8,32]{0,2,1:T(8,128)S(1)} %get-tuple-element.31, f32[64,8,32]{0,2,1:T(8,128)S(1)} %get-tuple-element.32, ...), kind=kLoop, calls=%fused_computation.130 | loop fusion | flops 20963328 | bytes 5013504 | tf_op jit(solution)/shard_map/reduce_sum | solution.py:107
  196.9 6.2 %fusion.75 = f32[32,8,32]{2,1,0:T(8,128)S(1)} fusion(f32[64,32,8]{0,2,1:T(8,128)S(1)} %bitcast.382, f32[64,32,8]{0,2,1:T(8,128)S(1)} %bitcast.378, f32[64,8,32]{0,2,1:T(8,128)S(1)} %get-tuple-element.29, f32[64,8,32]{0,2,1:T(8,128)S(1)} %get-tuple-element.30, f32[64,8,32]{0,2,1:T(8,128)S(1)} %get-tuple-element.31, f32[64,8,32]{0,2,1:T(8,128)S(1)} %get-tuple-element.32, ...), kind=kLoop, calls=%fused_computation.133 | loop fusion | flops 20963328 | bytes 5013504 | tf_op jit(solution)/shard_map/reduce_sum | solution.py:107
  203.1 6.2 %fusion.59 = f32[32,8,32]{2,1,0:T(8,128)S(1)} fusion(f32[64,32,8]{0,2,1:T(8,128)S(1)} %bitcast.383, f32[64,32,8]{0,2,1:T(8,128)S(1)} %bitcast.379, f32[64,8,32]{0,2,1:T(8,128)S(1)} %get-tuple-element.29, f32[64,8,32]{0,2,1:T(8,128)S(1)} %get-tuple-element.30, f32[64,8,32]{0,2,1:T(8,128)S(1)} %get-tuple-element.31, f32[64,8,32]{0,2,1:T(8,128)S(1)} %get-tuple-element.32, ...), kind=kLoop, calls=%fused_computation.117 | loop fusion | flops 20963328 | bytes 5013504 | tf_op jit(solution)/shard_map/reduce_sum | solution.py:107
  209.3 10.7 %fusion.30 = f32[64,8,32]{0,2,1:T(8,128)} fusion(f32[32,8,32]{2,1,0:T(8,128)S(1)} %bitcast.315, f32[32,8,32]{2,1,0:T(8,128)S(1)} %bitcast.323, f32[32,8,32]{2,1,0:T(8,128)S(1)} %bitcast.331, f32[32,8,32]{2,1,0:T(8,128)S(1)} %bitcast.339, f32[32,8,32]{2,1,0:T(8,128)S(1)} %bitcast.347, f32[64,32,8]{0,2,1:T(8,128)S(1)} %bitcast.370, ...), kind=kLoop, calls=%fused_computation.88 | loop fusion | flops 22003712 | bytes 4784128 | tf_op jit(solution)/shard_map/reduce_sum | solution.py:105
  220.1 10.7 %fusion.21 = f32[64,8,32]{0,2,1:T(8,128)} fusion(f32[32,8,32]{2,1,0:T(8,128)S(1)} %bitcast.316, f32[32,8,32]{2,1,0:T(8,128)S(1)} %bitcast.324, f32[32,8,32]{2,1,0:T(8,128)S(1)} %bitcast.332, f32[32,8,32]{2,1,0:T(8,128)S(1)} %bitcast.340, f32[32,8,32]{2,1,0:T(8,128)S(1)} %bitcast.348, f32[64,32,8]{0,2,1:T(8,128)S(1)} %bitcast.371, ...), kind=kLoop, calls=%fused_computation.79 | loop fusion | flops 22003712 | bytes 4784128 | tf_op jit(solution)/shard_map/reduce_sum | solution.py:105
  230.8 1.6 stack.75
  232.4 1.0 reshape_reshape.7
  233.4 4.0 %all-to-all-start.3 = ((f32[8,4,8,256]{3,2,1,0:T(8,128)}), f32[8,4,8,256]{3,2,1,0:T(8,128)S(1)}, u32[]{:S(2)}, u32[]{:S(2)}) async-start(f32[8,4,8,256]{3,2,1,0:T(8,128)} %reshape_reshape.7), calls=%async_computation.3 | async-start | bytes 524288 | tf_op jit(solution)/shard_map/all_to_all | solution.py:29
  237.5 0.9 bitcast_dynamic-update-slice_fusion.7
  238.4 0.9 bitcast_dynamic-update-slice_fusion.6
  239.4 0.9 bitcast_dynamic-update-slice_fusion.4
  240.4 1.8 copy.50
  242.2 1.4 reshape_reshape.6
  243.7 6.2 %all-to-all-start.2 = ((f32[16,4,8,256]{3,2,1,0:T(8,128)}), f32[16,4,8,256]{3,2,1,0:T(8,128)S(1)}, u32[]{:S(2)}, u32[]{:S(2)}) async-start(f32[16,4,8,256]{3,2,1,0:T(8,128)} %reshape_reshape.6), calls=%async_computation.2 | async-start | bytes 1048576 | tf_op jit(solution)/shard_map/all_to_all | solution.py:29
  250.0 0.6 gather_fusion.3
  250.7 0.7 fusion.84
  251.4 9.7 %all-to-all-done.2 = f32[16,4,8,256]{3,2,1,0:T(8,128)S(1)} async-done(((f32[16,4,8,256]{3,2,1,0:T(8,128)}), f32[16,4,8,256]{3,2,1,0:T(8,128)S(1)}, u32[]{:S(2)}, u32[]{:S(2)}) %all-to-all-start.2) | async-done | bytes 524320 | tf_op jit(solution)/shard_map/all_to_all | solution.py:29
  261.2 0.7 fusion.83
  262.1 3.5 %copy.52 = f32[128,1,4096]{2,1,0:T(1,128)} copy(f32[128,1,4096]{2,0,1:T(8,128)S(1)} %maximum_bitcast_fusion) | data formatting | bytes 4194304 | tf_op jit(solution)/shard_map/all_to_all | solution.py:41
  265.6 5.4 %all-to-all-start.4 = ((f32[128,1,4096]{2,1,0:T(1,128)}), f32[128,1,4096]{2,1,0:T(1,128)S(1)}, u32[]{:S(2)}, u32[]{:S(2)}) async-start(f32[128,1,4096]{2,1,0:T(1,128)} %copy.52), calls=%async_computation.4 | async-start | bytes 4194304 | tf_op jit(solution)/shard_map/all_to_all | solution.py:41
  271.0 2.4 scatter_custom_fusion
  273.4 0.6 gather_fusion.2
  274.1 27.0 %all-to-all-done.4 = f32[128,1,4096]{2,1,0:T(1,128)S(1)} async-done(((f32[128,1,4096]{2,1,0:T(1,128)}), f32[128,1,4096]{2,1,0:T(1,128)S(1)}, u32[]{:S(2)}, u32[]{:S(2)}) %all-to-all-start.4) | async-done | bytes 2097184 | tf_op jit(solution)/shard_map/all_to_all | solution.py:41
  301.1 1.6 copy.66
  303.6 0.6 copy.67
  (58 shorter events, 2.4 us)
Async XLA Ops:
  23.4 4.7 %copy-start.9 = (s32[64,32,1]{0,2,1:T(1,128)S(1)}, s32[64,32,1]{0,2,1:T(1,128)}, u32[]{:S(2)}) copy-start(s32[64,32,1]{0,2,1:T(1,128)} %param.10) | copy-start | bytes 24580
  23.4 52.9 %all-to-all-start.1 = ((f32[8,64,8,256]{3,2,1,0:T(8,128)}), f32[8,64,8,256]{3,2,1,0:T(8,128)}, u32[]{:S(2)}, u32[]{:S(2)}) async-start(f32[8,64,8,256]{3,2,1,0:T(8,128)} %stack.57), calls=%async_computation.1 | async-start | bytes 8388608 | tf_op jit(solution)/shard_map/all_to_all | solution.py:148
  28.1 17.5 %copy-start.1 = (s32[512]{0:T(512)S(1)}, s32[512]{0:T(512)}, u32[]{:S(2)}) copy-start(s32[512]{0:T(512)} %param.11) | copy-start | bytes 6148
  28.1 18.4 %copy-start.2 = (bf16[64,32,8,1,8]{0,4,3,2,1:T(8,128)(2,1)S(1)}, bf16[64,32,8,1,8]{0,4,3,2,1:T(8,128)(2,1)}, u32[]{:S(2)}) copy-start(bf16[64,32,8,1,8]{0,4,3,2,1:T(8,128)(2,1)} %param.9) | copy-start | bytes 786436
  79.7 17.0 %copy-start = (bf16[64,32,8,1,256]{0,4,2,1,3:T(8,128)(2,1)S(1)}, bf16[64,32,8,1,256]{0,4,2,1,3:T(8,128)(2,1)}, u32[]{:S(2)}) copy-start(bf16[64,32,8,1,256]{0,4,2,1,3:T(8,128)(2,1)} %copy.42) | copy-start | bytes 25165828
  116.1 36.1 %slice-start = ((s8[16777216]{0:T(1024)(128)(4,1)}), s8[4194304]{0:T(1024)(128)(4,1)S(1)}, s32[]{:S(2)}) async-start(s8[16777216]{0:T(1024)(128)(4,1)} %bitcast.258), calls=%async_computation.5 | async-start | bytes 8388608
  116.1 36.1 %slice-start.1 = ((s8[16777216]{0:T(1024)(128)(4,1)}), s8[4194304]{0:T(1024)(128)(4,1)S(1)}, s32[]{:S(2)}) async-start(s8[16777216]{0:T(1024)(128)(4,1)} %bitcast.258), calls=%async_computation.6 | async-start | bytes 8388608
  127.9 24.3 %slice-start.2 = ((s8[16777216]{0:T(1024)(128)(4,1)}), s8[4194304]{0:T(1024)(128)(4,1)S(1)}, s32[]{:S(2)}) async-start(s8[16777216]{0:T(1024)(128)(4,1)} %bitcast.258), calls=%async_computation.7 | async-start | bytes 8388608
  140.4 11.9 %slice-start.3 = ((s8[16777216]{0:T(1024)(128)(4,1)}), s8[4194304]{0:T(1024)(128)(4,1)S(1)}, s32[]{:S(2)}) async-start(s8[16777216]{0:T(1024)(128)(4,1)} %bitcast.258), calls=%async_computation.8 | async-start | bytes 8388608
  220.1 10.7 %copy-start.3 = (f32[32,8,32]{2,1,0:T(8,128)S(1)}, f32[32,8,32]{2,1,0:T(8,128)}, u32[]{:S(2)}) copy-start(f32[32,8,32]{2,1,0:T(8,128)} %fusion.66) | copy-start | bytes 98308
  220.1 10.7 %copy-start.4 = (f32[32,8,32]{2,1,0:T(8,128)S(1)}, f32[32,8,32]{2,1,0:T(8,128)}, u32[]{:S(2)}) copy-start(f32[32,8,32]{2,1,0:T(8,128)} %fusion.53) | copy-start | bytes 98308
  220.1 10.7 %copy-start.5 = (f32[32,8,32]{2,1,0:T(8,128)S(1)}, f32[32,8,32]{2,1,0:T(8,128)}, u32[]{:S(2)}) copy-start(f32[32,8,32]{2,1,0:T(8,128)} %fusion.50) | copy-start | bytes 98308
  230.8 8.6 %copy-start.8 = (f32[64,8,32]{0,2,1:T(8,128)S(1)}, f32[64,8,32]{0,2,1:T(8,128)}, u32[]{:S(2)}) copy-start(f32[64,8,32]{0,2,1:T(8,128)} %fusion.18) | copy-start | bytes 196612
  230.8 9.5 %copy-start.7 = (f32[64,8,32]{0,2,1:T(8,128)S(1)}, f32[64,8,32]{0,2,1:T(8,128)}, u32[]{:S(2)}) copy-start(f32[64,8,32]{0,2,1:T(8,128)} %fusion.36) | copy-start | bytes 196612
  230.8 9.6 %copy-start.6 = (f32[64,8,32]{0,2,1:T(8,128)S(1)}, f32[64,8,32]{0,2,1:T(8,128)}, u32[]{:S(2)}) copy-start(f32[64,8,32]{0,2,1:T(8,128)} %fusion.24) | copy-start | bytes 196612
  233.4 10.3 %all-to-all-start.3 = ((f32[8,4,8,256]{3,2,1,0:T(8,128)}), f32[8,4,8,256]{3,2,1,0:T(8,128)S(1)}, u32[]{:S(2)}, u32[]{:S(2)}) async-start(f32[8,4,8,256]{3,2,1,0:T(8,128)} %reshape_reshape.7), calls=%async_computation.3 | async-start | bytes 524288 | tf_op jit(solution)/shard_map/all_to_all | solution.py:29
  243.7 17.4 %all-to-all-start.2 = ((f32[16,4,8,256]{3,2,1,0:T(8,128)}), f32[16,4,8,256]{3,2,1,0:T(8,128)S(1)}, u32[]{:S(2)}, u32[]{:S(2)}) async-start(f32[16,4,8,256]{3,2,1,0:T(8,128)} %reshape_reshape.6), calls=%async_computation.2 | async-start | bytes 1048576 | tf_op jit(solution)/shard_map/all_to_all | solution.py:29
  265.6 35.5 %all-to-all-start.4 = ((f32[128,1,4096]{2,1,0:T(1,128)}), f32[128,1,4096]{2,1,0:T(1,128)S(1)}, u32[]{:S(2)}, u32[]{:S(2)}) async-start(f32[128,1,4096]{2,1,0:T(1,128)} %copy.52), calls=%async_computation.4 | async-start | bytes 4194304 | tf_op jit(solution)/shard_map/all_to_all | solution.py:41
